TPU v7x, 32 devices: a whole 2x2x4 slice. The times are simulated.
32 devices in a mesh: rep: 4 (over z), tp: 8 (over y, x, core).
Axes of the slice: x: 2, y: 2, z: 4, core: 2. Of those that a mesh axis runs over, the one named last changes fastest.
Arguments:
- attn: bfloat16 [3072, 4096], P('rep', 'tp'), parts along dimension 0, may hold values from -6 to 6
- output_weight: bfloat16 [4096, 8192], P(None, 'tp'), may hold values from -0.09375 to 0.09375
- adapter_down_weight: bfloat16 [8, 64, 4096], P('tp'), may hold values from -0.09375 to 0.09375
- adapter_up_weight: bfloat16 [8, 64, 8192], P('tp'), may hold values from -0.75 to 0.75
- block_adapter_index: int32 [24], P('rep'), parts along dimension 0, may hold values from 0 to 7
- adapter_page_table: int32 [8], replicated, may hold values from 0 to 7, each once
Outputs:
- projected: bfloat16 [3072, 8192], P('rep', 'tp'), parts along dimension 0
There are 4 independent parts, one for each index of `rep`. A program takes and returns all parts, laid end to end along the dimension named above; an argument that names none is the same for every part. Nothing has to cross between parts.
Inputs may be any that keep to these rules, and one draw needn't show every extreme that they name: adapter_page_table is a permutation; adapter a is stored on tp device adapter_page_table[a] (each device holds exactly one adapter), and row adapter_page_table[a] of adapter_down_weight and adapter_up_weight holds it. `block_adapter_index`: the adapter used by all 128 tokens of a block.
All inputs are finite; a program needn't handle non-finite values.
Results may differ from a plain program's by a relative error of at most 0.0046.
Values may be sent and summed in bfloat16 or wider, within the bound.
A program may use at most 64 MiB of HBM per device.

v0:
```python
import functools

import jax
import jax.numpy as jnp
from jax import lax
from jax.experimental import pallas as pl
from jax.experimental.pallas import tpu as pltpu
from jax.sharding import PartitionSpec as P

adapter_scale = 2.0
MESH = pl.DeviceIdType.MESH


def plain_shards(
    attn,
    output_weight,
    adapter_down_weight,
    adapter_up_weight,
    block_adapter_index,
    adapter_page_table,
):
    tokens = attn.shape[0]
    blocks = block_adapter_index.shape[0]
    block_rows = tokens // blocks
    page_slot_count = adapter_down_weight.shape[0]
    width_out = output_weight.shape[1]
    position = lax.axis_index("tp")
    block_page_index = adapter_page_table[block_adapter_index]
    up_weight_columns = lax.all_to_all(
        adapter_up_weight, "tp", split_axis=2, concat_axis=0, tiled=True
    )
    block_up = up_weight_columns[block_page_index]
    gathered = lax.all_gather(attn, "tp", axis=1, tiled=True)
    base_output = jnp.dot(gathered, output_weight, preferred_element_type=jnp.float32)
    row_blocks = gathered.reshape(blocks, block_rows, gathered.shape[1])
    side_sum = jnp.einsum(
        "btf,srf->bsrt", row_blocks, adapter_down_weight, preferred_element_type=jnp.float32
    )
    own_pages = position * page_slot_count + jnp.arange(page_slot_count, dtype=jnp.int32)
    owned = (block_page_index[:, None] == own_pages[None, :]).astype(jnp.float32)
    local_term = jnp.sum(owned[:, :, None, None] * side_sum, axis=1)
    shrunk = lax.psum(local_term.astype(jnp.bfloat16), "tp")
    adapter_output = jnp.einsum(
        "brt,brc->btc", shrunk, block_up, preferred_element_type=jnp.float32
    )
    adapter_output = adapter_output.reshape(tokens, width_out)
    return (base_output + adapter_scale * adapter_output).astype(jnp.bfloat16)


depth = 3


def link_orders(blocks):
    x_order, y_order = [(False, 1), (False, 0), (False, 3)], [(False, 0), (False, 1), (False, 2)]
    for s in range(blocks // 2):
        x_order.append((True, 2 * s))
        y_order.append((True, 2 * s + 1))
        for order, b in ((x_order, 2 * s + 2), (x_order, 2 * s + 5), (y_order, 2 * s + 3), (y_order, 2 * s + 4)):
            if b < blocks:
                order.append((False, b))
    return x_order, y_order


def kernel(
    n,
    reps,
    index_ref,
    table_ref,
    attn_ref,
    weight_ref,
    down_ref,
    up_ref,
    out_ref,
    a_all,
    w_all,
    acc,
    out_stage,
    dn_all,
    up_all,
    part,
    half_in,
    chip_part,
    part_in,
    sum_all,
    send_sem,
    recv_sem,
    local_sem,
):
    blocks = index_ref.shape[0]
    rows = a_all.shape[1] // blocks
    rank = dn_all.shape[1]
    f_own = a_all.shape[2]
    c_own = up_all.shape[2]
    share = rank // reps
    red = rank // n
    me = lax.axis_index("tp")
    z = lax.axis_index("rep")
    core = lax.rem(me, 2)
    x_at = lax.rem(me // 2, 2)
    y_at = me // 4
    mate = me + 1 - 2 * core
    xn = me + 2 - 4 * x_at
    yn = me + 4 - 8 * y_at
    dg = xn + 4 - 8 * y_at

    def mate_of(d):
        return d + 1 - 2 * core

    counts = [0, 0]
    sends = []

    def remote(src, dst, axis, target):
        k = counts[0]
        counts[0] += 1
        copy = pltpu.make_async_remote_copy(
            src_ref=src,
            dst_ref=dst,
            send_sem=send_sem.at[k],
            recv_sem=recv_sem.at[k],
            device_id={axis: target},
            device_id_type=MESH,
        )
        copy.start()
        sends.append(copy)
        return copy

    def local(src, dst):
        k = counts[1]
        counts[1] += 1
        copy = pltpu.make_async_copy(src, dst, local_sem.at[k])
        copy.start()
        return copy

    own_load = local(attn_ref, a_all.at[me])
    z_rows = pl.ds(pl.multiple_of(z * share, share), share)
    own_f = pl.ds(pl.multiple_of(me * f_own, f_own), f_own)
    own_c = pl.ds(pl.multiple_of(me * c_own, c_own), c_own)
    own_dn = local(down_ref.at[0, :, own_f], dn_all.at[me])
    own_up = local(up_ref.at[0, z_rows, own_c], up_all.at[me, z_rows, :])

    barrier = pltpu.get_barrier_semaphore()
    for d in range(1, n):
        pl.semaphore_signal(
            barrier, inc=1, device_id={"tp": lax.rem(me + d, n)}, device_id_type=MESH
        )
    for d in range(1, reps):
        pl.semaphore_signal(
            barrier, inc=1, device_id={"rep": lax.rem(z + d, reps)}, device_id_type=MESH
        )
    pl.semaphore_wait(barrier, n - 1 + reps - 1)

    dn_copies, up_copies = [], []
    for d in range(1, n):
        j = lax.rem(me + d, n)
        cols = pl.ds(pl.multiple_of(j * f_own, f_own), f_own)
        dn_copies.append(
            remote(down_ref.at[0, :, cols], dn_all.at[me], "tp", j)
        )
    for d in range(1, n):
        j = lax.rem(me + d, n)
        cols = pl.ds(pl.multiple_of(j * c_own, c_own), c_own)
        up_copies.append(
            remote(up_ref.at[0, z_rows, cols], up_all.at[me, z_rows, :], "tp", j)
        )

    own_load.wait()

    def chunk(slot, b):
        return a_all.at[slot, pl.ds(b * rows, rows), :]

    x_order, y_order = link_orders(blocks)
    x_copies, y_copies, x_mate, y_mate = [], [], {}, {}

    def issue(k):
        if k < len(x_order):
            passed, b = x_order[k]
            slot = yn if passed else me
            x_copies.append(remote(chunk(slot, b), chunk(slot, b), "tp", xn))
            passed, b = y_order[k]
            slot = xn if passed else me
            y_copies.append(remote(chunk(slot, b), chunk(slot, b), "tp", yn))

    def event(k):
        x_copies[k].wait_recv()
        y_copies[k].wait_recv()
        issue(k + depth)
        passed, b = x_order[k]
        slot = dg if passed else xn
        x_mate[passed, b] = remote(chunk(slot, b), chunk(slot, b), "tp", mate)
        passed, b = y_order[k]
        slot = dg if passed else yn
        y_mate[passed, b] = remote(chunk(slot, b), chunk(slot, b), "tp", mate)

    issue(0)
    mate_copy = remote(a_all.at[me], a_all.at[me], "tp", mate)
    issue(1)

    w_loads = [local(weight_ref.at[pl.ds(pl.multiple_of(s * f_own, f_own), f_own), :], w_all.at[s])
               for s in (me, mate, xn, mate_of(xn), yn, mate_of(yn), dg, mate_of(dg))]

    width = acc.shape[1]
    tile = 256
    pair = 2 * rows
    pairs = blocks // 2

    def multiply(s, slots, fresh=False):
        at = pl.ds(s * pair, pair)

        @pl.loop(0, width // tile)
        def _(t):
            cols = pl.ds(pl.multiple_of(t * tile, tile), tile)
            total = None if fresh else acc[at, cols]
            for slot in slots:
                term = jnp.dot(
                    a_all[slot, at, :], w_all[slot, :, cols], preferred_element_type=jnp.float32
                )
                total = term if total is None else total + term
            acc[at, cols] = total

    def multiply_sides(s):
        for b in (2 * s, 2 * s + 1):
            x_mate[False, b].wait_recv()
            y_mate[False, b].wait_recv()
        multiply(s, (xn, mate_of(xn), yn, mate_of(yn)))

    def multiply_diagonal(s):
        x_mate[True, 2 * s].wait_recv()
        y_mate[True, 2 * s + 1].wait_recv()
        multiply(s, (dg, mate_of(dg)))

    half = rank // 2
    my_half = pl.ds(pl.multiple_of(core * half, half), half)
    mate_half = pl.ds(pl.multiple_of((1 - core) * half, half), half)

    def piece(device):
        return pl.ds(pl.multiple_of(core * half + (device // 2) * red, red), red)

    peers = (xn, yn, dg)

    def pages(b):
        return table_ref[index_ref[b]]

    own_dn.wait()
    for copy in dn_copies:
        copy.wait_recv()
    for b in range(blocks):
        part[b] = lax.dot_general(
            dn_all[pages(b)],
            a_all[me, pl.ds(b * rows, rows), :],
            (((1,), (1,)), ((), ())),
            preferred_element_type=jnp.float32,
        )
    half_copy = remote(part.at[:, mate_half, :], half_in, "tp", mate)
    mate_copy.wait_recv()
    w_loads[0].wait()
    w_loads[1].wait()
    multiply(0, (me, mate), True)
    half_copy.wait_recv()
    chip_part[:, my_half, :] = part[:, my_half, :] + half_in[...]
    part_copies = [
        remote(chip_part.at[:, piece(p), :], part_in.at[i], "tp", p) for i, p in enumerate(peers)
    ]
    issue(2)
    own_up.wait()
    for copy in up_copies:
        copy.wait_recv()
    up_z = [
        remote(up_all.at[:, z_rows, :], up_all.at[:, z_rows, :], "rep", lax.rem(z + d, reps))
        for d in range(1, reps)
    ]
    event(0)
    multiply(1, (me, mate), True)
    event(1)
    for s in range(2, pairs):
        multiply(s, (me, mate), True)
    for load in w_loads[2:]:
        load.wait()
    event(2)
    total = chip_part[:, piece(me), :]
    for i in range(len(peers)):
        part_copies[i].wait_recv()
        total = total + part_in[i]
    sum_all[:, piece(me), :] = total
    sum_copies = [
        remote(sum_all.at[:, piece(me), :], sum_all.at[:, piece(me), :], "tp", p) for p in peers
    ]
    multiply_sides(0)

    event(3)
    event(4)
    multiply_sides(1)
    event(5)
    multiply_diagonal(0)
    event(6)
    for copy in sum_copies:
        copy.wait_recv()
    sum_mate = remote(sum_all.at[:, my_half, :], sum_all.at[:, my_half, :], "tp", mate)
    multiply_diagonal(1)
    event(7)
    sum_mate.wait_recv()
    for copy in up_z:
        copy.wait_recv()
    for b in range(blocks):
        at = pl.ds(b * rows, rows)
        adapted = lax.dot_general(
            sum_all[b].astype(jnp.bfloat16),
            up_all[pages(b)],
            (((0,), (0,)), ((), ())),
            preferred_element_type=jnp.float32,
        )
        acc[at, :] += adapter_scale * adapted
    multiply_sides(pairs - 1)
    out_copies = []
    for s in range(pairs - 1):
        at = pl.ds(s * pair, pair)
        out_stage[at, :] = acc[at, :].astype(out_stage.dtype)
        out_copies.append(local(out_stage.at[at, :], out_ref.at[at, :]))
    event(8)
    last = pairs - 1
    multiply(last, (dg,))
    x_mate[True, 2 * last].wait_recv()
    y_mate[True, 2 * last + 1].wait_recv()
    at = pl.ds(last * pair, pair)

    @pl.loop(0, width // tile)
    def _(t):
        cols = pl.ds(pl.multiple_of(t * tile, tile), tile)
        slot = mate_of(dg)
        total = acc[at, cols] + jnp.dot(
            a_all[slot, at, :], w_all[slot, :, cols], preferred_element_type=jnp.float32
        )
        out_stage[at, cols] = total.astype(out_stage.dtype)

    out_copies.append(local(out_stage.at[at, :], out_ref.at[at, :]))
    for copy in sends:
        copy.wait_send()
    for copy in out_copies:
        copy.wait()


def shards(n, reps, attn, weight, down, up, index, table):
    tokens, f_own = attn.shape
    blocks = index.shape[0]
    rows = tokens // blocks
    features, width = weight.shape
    rank = down.shape[1]
    copies = 2 * (n - 1) + 1 + 3 * blocks + (reps - 1) + 3 * blocks + 2 * (n // 2 - 1) + 2
    return pl.pallas_call(
        functools.partial(kernel, n, reps),
        out_shape=jax.ShapeDtypeStruct((tokens, width), jnp.bfloat16),
        in_specs=[pl.BlockSpec(memory_space=pltpu.SMEM)] * 2
        + [pl.BlockSpec(memory_space=pl.ANY)] * 4,
        out_specs=pl.BlockSpec(memory_space=pl.ANY),
        scratch_shapes=[
            pltpu.VMEM((n, tokens, f_own), jnp.bfloat16),
            pltpu.VMEM((n, features // n, width), jnp.bfloat16),
            pltpu.VMEM((tokens, width), jnp.float32),
            pltpu.VMEM((tokens, width), jnp.bfloat16),
            pltpu.VMEM((n, rank, f_own), jnp.bfloat16),
            pltpu.VMEM((n, rank, width), jnp.bfloat16),
            pltpu.VMEM((blocks, rank, rows), jnp.float32),
            pltpu.VMEM((blocks, rank // 2, rows), jnp.float32),
            pltpu.VMEM((blocks, rank, rows), jnp.float32),
            pltpu.VMEM((n // 2 - 1, blocks, rank // n, rows), jnp.float32),
            pltpu.VMEM((blocks, rank, rows), jnp.float32),
            pltpu.SemaphoreType.DMA((copies,)),
            pltpu.SemaphoreType.DMA((copies,)),
            pltpu.SemaphoreType.DMA((3 + n + blocks // 2,)),
        ],
        compiler_params=pltpu.CompilerParams(
            collective_id=0, has_side_effects=True, vmem_limit_bytes=60 * 1024 * 1024
        ),
    )(index, table, attn, weight, down, up)


def solution(mesh):
    n, reps = mesh.shape["tp"], mesh.shape["rep"]

    def body(attn, weight, down, up, index, table):
        blocks = index.shape[0]
        fits = (
            n == 8
            and reps > 1
            and blocks % 2 == 0
            and blocks == 6
            and down.shape[0] == 1
            and down.shape[1] % (16 * reps) == 0
            and down.shape[1] % (8 * n) == 0
            and attn.shape[0] % (128 * blocks) == 0
            and attn.shape[1] % 128 == 0
            and weight.shape[1] % 256 == 0
        )
        if fits:
            return shards(n, reps, attn, weight, down, up, index, table)
        return plain_shards(attn, weight, down, up, index, table)

    return jax.shard_map(
        body,
        mesh=mesh,
        in_specs=(
            P("rep", "tp"),
            P(None, "tp"),
            P("tp", None, None),
            P("tp", None, None),
            P("rep"),
            P(),
        ),
        out_specs=P("rep", "tp"),
        check_vma=False,
    )
```

profile of v0, /device:TPU:0, one launch (start us, length us, event | category | flops | bytes accessed | tf_op | source)
XLA Modules:
  0.0 52.3 jit_solution(14367214812615805115)
XLA Ops:
  0.0 49.6 %shard_map.64 = bf16[768,1024]{1,0:T(8,128)(2,1)} custom-call(s32[6]{0:T(128)} %index_ref.1, s32[8]{0:T(128)} %table_ref.1, bf16[768,512]{1,0:T(8,128)(2,1)} %attn_ref.1, bf16[4096,1024]{1,0:T(8,128)(2,1)} %weight_ref.1, bf16[1,64,4096]{2,1,0:T(8,128)(2,1)} %down_ref.1, bf16[1,64,8192]{2,1,0:T(8,128)(2,1)} %up_ref.1), custom_call_target="tpu_custom_call" | custom-call | tf_op jit(solution)/shard_map/pallas_call | solution.py:348
  49.6 2.7 %copy.8 = bf16[768,1024]{1,0:T(8,128)(2,1)} copy(bf16[768,1024]{1,0:T(8,128)(2,1)} %shard_map.64) | data formatting | bytes 3145728
where the time goes:
time: 52.5 us; the launch traced here: 52.3 us
  Pallas kernels  49.6 us (94%)
  local copies, waits for them, and re-layouts  2.67 us (5%)
    pallas_call x1, Pallas kernels, shards(): pl.pallas_call(functools.partial(kernel, n, reps), out_shape=jax.ShapeDty...  49.6 us
    unnamed x1, local copies, waits for them, and re-layouts  2.67 us

commit v1 on v0

v1 whole, which is shorter than its diff:
```python
import functools

import jax
import jax.numpy as jnp
from jax import lax
from jax.experimental import pallas as pl
from jax.experimental.pallas import tpu as pltpu
from jax.sharding import PartitionSpec as P

adapter_scale = 2.0
MESH = pl.DeviceIdType.MESH


def plain_shards(
    attn,
    output_weight,
    adapter_down_weight,
    adapter_up_weight,
    block_adapter_index,
    adapter_page_table,
):
    tokens = attn.shape[0]
    blocks = block_adapter_index.shape[0]
    block_rows = tokens // blocks
    page_slot_count = adapter_down_weight.shape[0]
    width_out = output_weight.shape[1]
    position = lax.axis_index("tp")
    block_page_index = adapter_page_table[block_adapter_index]
    up_weight_columns = lax.all_to_all(
        adapter_up_weight, "tp", split_axis=2, concat_axis=0, tiled=True
    )
    block_up = up_weight_columns[block_page_index]
    gathered = lax.all_gather(attn, "tp", axis=1, tiled=True)
    base_output = jnp.dot(gathered, output_weight, preferred_element_type=jnp.float32)
    row_blocks = gathered.reshape(blocks, block_rows, gathered.shape[1])
    side_sum = jnp.einsum(
        "btf,srf->bsrt", row_blocks, adapter_down_weight, preferred_element_type=jnp.float32
    )
    own_pages = position * page_slot_count + jnp.arange(page_slot_count, dtype=jnp.int32)
    owned = (block_page_index[:, None] == own_pages[None, :]).astype(jnp.float32)
    local_term = jnp.sum(owned[:, :, None, None] * side_sum, axis=1)
    shrunk = lax.psum(local_term.astype(jnp.bfloat16), "tp")
    adapter_output = jnp.einsum(
        "brt,brc->btc", shrunk, block_up, preferred_element_type=jnp.float32
    )
    adapter_output = adapter_output.reshape(tokens, width_out)
    return (base_output + adapter_scale * adapter_output).astype(jnp.bfloat16)


depth = 4
split = 2
z_parts = 2


def link_orders(chunks):
    x_order, y_order = [(False, 1), (False, 0), (False, 3)], [(False, 0), (False, 1), (False, 2)]
    for s in range(chunks // 2):
        x_order.append((True, 2 * s))
        y_order.append((True, 2 * s + 1))
        for order, b in ((x_order, 2 * s + 2), (x_order, 2 * s + 5), (y_order, 2 * s + 3), (y_order, 2 * s + 4)):
            if b < chunks:
                order.append((False, b))
    return x_order, y_order


def semaphore_counts(blocks, reps):
    sends = 9 + 5 + 2 * z_parts * (reps - 1)
    receives = 3 * blocks * split // 2 + 2 * blocks + 8 + 2 * z_parts * (reps - 1)
    return sends, receives


def kernel(
    n,
    reps,
    index_ref,
    table_ref,
    attn_ref,
    weight_ref,
    down_ref,
    up_ref,
    out_ref,
    a_all,
    w_all,
    acc,
    dn_own,
    up_own,
    dn_all,
    up_all,
    part,
    half_in,
    chip_part,
    x_out,
    x_in,
    y_out,
    y_in,
    sum_all,
    send_sem,
    recv_sem,
    local_sem,
    far_sem,
):
    blocks = index_ref.shape[0]
    chunks = blocks * split
    rows = a_all.shape[1] // blocks
    chunk_rows = rows // split
    rank = dn_all.shape[1]
    f_own = a_all.shape[2]
    c_own = up_all.shape[2]
    width = acc.shape[1]
    me = lax.axis_index("tp")
    z = lax.axis_index("rep")
    core = lax.rem(me, 2)
    x_at = lax.rem(me // 2, 2)
    y_at = me // 4
    mate = me + 1 - 2 * core
    xn = me + 2 - 4 * x_at
    yn = me + 4 - 8 * y_at
    dg = xn + 4 - 8 * y_at
    zp = z + 1 - 2 * lax.rem(z, 2)

    def mate_of(d):
        return d + 1 - 2 * core

    counts = {"send": 0, "recv": 0, "local": 0}

    def take(kind, many=1):
        k = counts[kind]
        counts[kind] += many
        return k

    def remote(src, dst, axis, target, s, r):
        return pltpu.make_async_remote_copy(
            src_ref=src,
            dst_ref=dst,
            send_sem=send_sem.at[s],
            recv_sem=recv_sem.at[r],
            device_id={axis: target},
            device_id_type=MESH,
        )

    def drain(sem, ref):
        pltpu.make_async_copy(ref, ref, sem).wait()

    singles = []

    def single(src, dst, axis, target):
        copy = remote(src, dst, axis, target, take("send"), take("recv"))
        copy.start()
        singles.append(copy)
        return copy

    def local(src, dst, k=None):
        copy = pltpu.make_async_copy(src, dst, local_sem.at[take("local") if k is None else k])
        copy.start()
        return copy

    quarter = rank // reps
    pair_rank = rank // 2

    def quarter_of(at):
        return pl.ds(pl.multiple_of(at * quarter, quarter), quarter)

    up_rows = quarter_of(z)
    dn_rows = pl.ds(pl.multiple_of(lax.rem(z, 2) * pair_rank, pair_rank), pair_rank)
    own_f = pl.ds(pl.multiple_of(me * f_own, f_own), f_own)
    own_c = pl.ds(pl.multiple_of(me * c_own, c_own), c_own)

    dn_stage = local(down_ref.at[0, dn_rows, :], dn_own)
    up_stage = local(up_ref.at[0, up_rows, :], up_own)
    own_load = local(attn_ref, a_all.at[me])
    own_dn = local(down_ref.at[0, dn_rows, own_f], dn_all.at[me, dn_rows, :])
    own_up = local(up_ref.at[0, up_rows, own_c], up_all.at[me, up_rows, :])

    barrier = pltpu.get_barrier_semaphore()
    near = (xn, yn, mate_of(xn), mate_of(yn), mate)
    for d in near:
        pl.semaphore_signal(barrier, inc=1, device_id={"tp": d}, device_id_type=MESH)

    @pl.when(z + 1 < reps)
    def _():
        pl.semaphore_signal(barrier, inc=1, device_id={"rep": z + 1}, device_id_type=MESH)

    @pl.when(z > 0)
    def _():
        pl.semaphore_signal(barrier, inc=1, device_id={"rep": z - 1}, device_id_type=MESH)

    z_near = jnp.where(z > 0, 1, 0) + jnp.where(z + 1 < reps, 1, 0)
    pl.semaphore_wait(barrier, len(near) + z_near)
    pl.semaphore_signal(far_sem, inc=1, device_id={"tp": xn}, device_id_type=MESH)

    dn_s, dn_r = take("send"), take("recv")
    up_s, up_r = take("send"), take("recv")

    def send_dn(j):
        cols = pl.ds(pl.multiple_of(j * f_own, f_own), f_own)
        remote(dn_own.at[:, cols], dn_all.at[me, dn_rows, :], "tp", j, dn_s, dn_r).start()

    def send_up(j):
        cols = pl.ds(pl.multiple_of(j * c_own, c_own), c_own)
        remote(up_own.at[:, cols], up_all.at[me, up_rows, :], "tp", j, up_s, up_r).start()

    dn_stage.wait()
    for j in near:
        send_dn(j)
    pl.semaphore_wait(far_sem, 1)
    for j in (dg, mate_of(dg)):
        send_dn(j)
    up_stage.wait()
    for j in near + (dg, mate_of(dg)):
        send_up(j)
    own_load.wait()

    def chunk(slot, b):
        return a_all.at[slot, pl.ds(b * chunk_rows, chunk_rows), :]

    x_order, y_order = link_orders(chunks)
    x_own, y_own, passed_on, x_pass, y_pass, d_pass = (take("send") for _ in range(6))
    event_r, side_r, diag_r = take("recv", len(x_order)), take("recv", blocks), take("recv", blocks)

    def issue(k):
        if k < len(x_order):
            passed, b = x_order[k]
            src = chunk(yn if passed else me, b)
            remote(src, src, "tp", xn, passed_on if passed else x_own, event_r + k).start()
            passed, b = y_order[k]
            src = chunk(xn if passed else me, b)
            remote(src, src, "tp", yn, passed_on if passed else y_own, event_r + k).start()

    issued = [0]

    def issue_up_to(k):
        while issued[0] < min(k + 1 + depth, len(x_order)):
            i = issued[0]
            (x_passed, x_b), (y_passed, y_b) = x_order[i], y_order[i]
            if x_passed and y_order.index((False, x_b)) > k:
                break
            if y_passed and x_order.index((False, y_b)) > k:
                break
            issue(i)
            issued[0] += 1

    def rows_of(many):
        return a_all.at[0, pl.ds(0, many * chunk_rows), :]

    def event(k):
        drain(recv_sem.at[event_r + k], rows_of(2))
        issue_up_to(k)
        for (passed, b), side, s in ((x_order[k], xn, x_pass), (y_order[k], yn, y_pass)):
            src = chunk(dg if passed else side, b)
            r = (diag_r if passed else side_r) + b // split
            remote(src, src, "tp", mate, d_pass if passed else s, r).start()

    mate_copy = single(a_all.at[me], a_all.at[me], "tp", mate)
    issue_up_to(-1)

    w_order = (me, mate, xn, mate_of(xn), yn, mate_of(yn), dg, mate_of(dg))
    w_k = take("local", 4)
    for i, s in enumerate(w_order):
        local(weight_ref.at[pl.ds(pl.multiple_of(s * f_own, f_own), f_own), :], w_all.at[s], w_k + i // 2)

    def w_wait(i):
        drain(local_sem.at[w_k + i], w_all.at[pl.ds(0, 2)])

    tile = 256

    def multiply(at, slots, fresh=False, final=False, unroll=False):
        @pl.loop(0, width // tile, unroll=unroll)
        def _(t):
            cols = pl.ds(pl.multiple_of(t * tile, tile), tile)
            total = None if fresh else acc[at, cols]
            for slot in slots:
                term = jnp.dot(
                    a_all[slot, at, :], w_all[slot, :, cols], preferred_element_type=jnp.float32
                )
                total = term if total is None else total + term
            if final:
                out_ref[at, cols] = total.astype(out_ref.dtype)
            else:
                acc[at, cols] = total

    def of_block(b):
        return pl.ds(b * rows, rows)

    def multiply_sides(b):
        drain(recv_sem.at[side_r + b], rows_of(2 * split))
        multiply(of_block(b), (xn, mate_of(xn), yn, mate_of(yn)))

    def wait_diagonal(b):
        drain(recv_sem.at[diag_r + b], rows_of(split))

    def multiply_diagonal(b, final=False):
        wait_diagonal(b)
        multiply(of_block(b), (dg, mate_of(dg)), final=final)

    half = rank // 2
    my_half = pl.ds(pl.multiple_of(core * half, half), half)
    mate_half = pl.ds(pl.multiple_of((1 - core) * half, half), half)

    def pages(b):
        return table_ref[index_ref[b]]

    own_pairs = blocks // 2
    mate_copy.wait_recv()
    w_wait(0)
    for s in range(own_pairs):
        multiply(pl.ds(s * 2 * rows, 2 * rows), (me, mate), fresh=True)
        if s == 0:
            own_dn.wait()
            drain(recv_sem.at[dn_r], dn_own.at[:, pl.ds(0, (n - 1) * f_own)])
            dn_z = single(dn_all.at[:, dn_rows, :], dn_all.at[:, dn_rows, :], "rep", zp)

    z_s, z_r = take("send", 2 * z_parts * (reps - 1)), take("recv", 2 * z_parts * (reps - 1))

    def up_piece(owner, right, step, h):
        pages_of = pl.ds(h * (n // z_parts), n // z_parts)
        piece = up_all.at[pages_of, quarter_of(owner), :]
        k = (step * 2 + (0 if right else 1)) * z_parts + h
        return remote(piece, piece, "rep", z + 1 if right else z - 1, z_s + k, z_r + k)

    def up_sends(right, step):
        return (z + 1 < reps) & (z >= step) if right else (z > 0) & (z + step < reps)

    def up_receives(right, step):
        return z > step if right else z + 1 + step < reps

    def up_owner(right, step):
        return z - step if right else z + step

    def up_start(step, h):
        for right in (True, False):
            @pl.when(up_sends(right, step))
            def _():
                up_piece(up_owner(right, step), right, step, h).start()

    def up_event(step, h):
        for right in (True, False):
            @pl.when(up_receives(right, step))
            def _():
                up_piece(up_owner(right, step), right, step, h).wait_recv()

        if step + 1 < reps - 1:
            up_start(step + 1, h)

    own_up.wait()
    drain(recv_sem.at[up_r], up_own.at[:, pl.ds(0, (n - 1) * c_own)])
    for h in range(z_parts):
        up_start(0, h)
    for i in range(1, 4):
        w_wait(i)

    event(0)
    event(1)
    event(2)
    multiply_sides(0)
    dn_z.wait_recv()
    for b in range(blocks):
        part[b] = lax.dot_general(
            dn_all[pages(b)],
            a_all[me, of_block(b), :],
            (((1,), (1,)), ((), ())),
            preferred_element_type=jnp.float32,
        )
    half_copy = single(part.at[:, mate_half, :], half_in, "tp", mate)
    event(3)
    event(4)
    half_copy.wait_recv()
    chip_part[...] = part[:, my_half, :] + half_in[...]
    x_out[...] = chip_part[...].astype(x_out.dtype)
    x_swap = single(x_out, x_in, "tp", xn)
    multiply_diagonal(0)
    event(5)
    up_event(0, 0)
    multiply_sides(1)
    event(6)
    multiply_diagonal(1)
    event(7)
    up_event(0, 1)
    event(8)
    multiply_sides(2)
    event(9)
    x_swap.wait_recv()
    chip_part[...] += x_in[...].astype(jnp.float32)
    y_out[...] = chip_part[...].astype(y_out.dtype)
    y_swap = single(y_out, y_in, "tp", yn)
    up_event(1, 0)
    event(10)
    multiply_diagonal(2)
    event(11)
    up_event(1, 1)
    multiply_sides(3)
    event(12)
    event(13)
    multiply_diagonal(3)
    event(14)
    multiply_sides(4)
    event(15)
    y_swap.wait_recv()
    sum_all[:, my_half, :] = (chip_part[...] + y_in[...].astype(jnp.float32)).astype(sum_all.dtype)
    sum_mate = single(sum_all.at[:, my_half, :], sum_all.at[:, my_half, :], "tp", mate)
    event(16)
    multiply_diagonal(blocks - 2)
    multiply_sides(blocks - 1)
    sum_mate.wait_recv()
    for h in range(z_parts):
        up_event(2, h)

    last = blocks - 1
    for b in range(blocks):
        at = of_block(b)
        adapted = lax.dot_general(
            sum_all[b],
            up_all[pages(b)],
            (((0,), (0,)), ((), ())),
            preferred_element_type=jnp.float32,
        )
        total = acc[at, :] + adapter_scale * adapted
        if b < last:
            out_ref[at, :] = total.astype(out_ref.dtype)
        else:
            acc[at, :] = total
    event(17)
    multiply(of_block(last), (dg,), unroll=True)
    wait_diagonal(last)
    multiply(of_block(last), (mate_of(dg),), final=True, unroll=True)

    for copy in singles:
        copy.wait_send()
    drain(send_sem.at[dn_s], dn_own.at[:, pl.ds(0, (n - 1) * f_own)])
    drain(send_sem.at[up_s], up_own.at[:, pl.ds(0, (n - 1) * c_own)])
    for s in (x_own, y_own, passed_on, x_pass, y_pass, d_pass):
        drain(send_sem.at[s], a_all.at[0])
    for step in range(reps - 1):
        for right in (True, False):
            @pl.when(up_sends(right, step))
            def _():
                for h in range(z_parts):
                    up_piece(up_owner(right, step), right, step, h).wait_send()


def shards(n, reps, attn, weight, down, up, index, table):
    tokens, f_own = attn.shape
    blocks = index.shape[0]
    rows = tokens // blocks
    features, width = weight.shape
    rank = down.shape[1]
    sends, receives = semaphore_counts(blocks, reps)
    half = (blocks, rank // 2, rows)
    return pl.pallas_call(
        functools.partial(kernel, n, reps),
        out_shape=pltpu.VMEM((tokens, width), jnp.bfloat16),
        in_specs=[pl.BlockSpec(memory_space=pltpu.SMEM)] * 2
        + [pl.BlockSpec(memory_space=pltpu.HBM)] * 4,
        out_specs=pl.BlockSpec(memory_space=pltpu.VMEM),
        scratch_shapes=[
            pltpu.VMEM((n, tokens, f_own), jnp.bfloat16),
            pltpu.VMEM((n, features // n, width), jnp.bfloat16),
            pltpu.VMEM((tokens, width), jnp.float32),
            pltpu.VMEM((rank // 2, features), jnp.bfloat16),
            pltpu.VMEM((rank // reps, n * width), jnp.bfloat16),
            pltpu.VMEM((n, rank, f_own), jnp.bfloat16),
            pltpu.VMEM((n, rank, width), jnp.bfloat16),
            pltpu.VMEM((blocks, rank, rows), jnp.float32),
            pltpu.VMEM(half, jnp.float32),
            pltpu.VMEM(half, jnp.float32),
            pltpu.VMEM(half, jnp.bfloat16),
            pltpu.VMEM(half, jnp.bfloat16),
            pltpu.VMEM(half, jnp.bfloat16),
            pltpu.VMEM(half, jnp.bfloat16),
            pltpu.VMEM((blocks, rank, rows), jnp.bfloat16),
            pltpu.SemaphoreType.DMA((sends,)),
            pltpu.SemaphoreType.DMA((receives,)),
            pltpu.SemaphoreType.DMA((9,)),
            pltpu.SemaphoreType.REGULAR,
        ],
        compiler_params=pltpu.CompilerParams(
            collective_id=0, has_side_effects=True, vmem_limit_bytes=60 * 1024 * 1024
        ),
    )(index, table, attn, weight, down, up)


def solution(mesh):
    n, reps = mesh.shape["tp"], mesh.shape["rep"]

    def body(attn, weight, down, up, index, table):
        blocks = index.shape[0]
        fits = (
            n == 8
            and reps == 4
            and blocks % 2 == 0
            and blocks == 6
            and down.shape[0] == 1
            and down.shape[1] % (16 * reps) == 0
            and down.shape[1] % (8 * n) == 0
            and attn.shape[0] % (128 * blocks) == 0
            and attn.shape[1] % 128 == 0
            and weight.shape[1] % 256 == 0
        )
        if fits:
            return shards(n, reps, attn, weight, down, up, index, table)
        return plain_shards(attn, weight, down, up, index, table)

    return jax.shard_map(
        body,
        mesh=mesh,
        in_specs=(
            P("rep", "tp"),
            P(None, "tp"),
            P("tp", None, None),
            P("tp", None, None),
            P("rep"),
            P(),
        ),
        out_specs=P("rep", "tp"),
        check_vma=False,
    )
```

time: 52.5 us -> 43.8 us (0.83)
  Pallas kernels: 49.6 us -> 42.5 us
  local copies, waits for them, and re-layouts: 2.67 us -> 1.15 us
    pallas_call x1, Pallas kernels: 49.6 us -> 42.5 us  [shards(): pl.pallas_call(functools.partial(kernel, n, reps), out_shape=pltpu.VMEM((...]
    unnamed x1, local copies, waits for them, and re-layouts: 2.67 us -> 1.15 us
where the time goes in v1:
time: 43.8 us; the launch traced here: 43.7 us
  Pallas kernels  42.5 us (97%)
  local copies, waits for them, and re-layouts  1.15 us (3%)
    pallas_call x1, Pallas kernels, shards(): pl.pallas_call(functools.partial(kernel, n, reps), out_shape=pltpu.VMEM((...  42.5 us
    unnamed x1, local copies, waits for them, and re-layouts  1.15 us

profile of v1, /device:TPU:0, one launch (start us, length us, event | category | flops | bytes accessed | tf_op | source)
XLA Modules:
  0.0 43.7 jit_solution(13221388960941539933)
XLA Ops:
  0.0 42.5 %shard_map.64 = bf16[768,1024]{1,0:T(8,128)(2,1)S(1)} custom-call(s32[6]{0:T(128)} %index_ref.1, s32[8]{0:T(128)} %table_ref.1, bf16[768,512]{1,0:T(8,128)(2,1)} %attn_ref.1, bf16[4096,1024]{1,0:T(8,128)(2,1)} %weight_ref.1, bf16[1,64,4096]{2,1,0:T(8,128)(2,1)} %down_ref.1, bf16[1,64,8192]{2,1,0:T(8,128)(2,1)} %up_ref.1), custom_call_target="tpu_custom_call" | custom-call | tf_op jit(solution)/shard_map/pallas_call | solution.py:448
  42.5 1.1 %copy.8 = bf16[768,1024]{1,0:T(8,128)(2,1)} copy(bf16[768,1024]{1,0:T(8,128)(2,1)S(1)} %shard_map.64) | data formatting | bytes 3145728

commit v2 on v1

--- a/solution.py
+++ b/solution.py
@@ -60,6 +60,14 @@
         for order, b in ((x_order, 2 * s + 2), (x_order, 2 * s + 5), (y_order, 2 * s + 3), (y_order, 2 * s + 4)):
             if b < chunks:
                 order.append((False, b))
+    x_order[-6:] = [
+        (False, chunks - 1), (True, chunks - 6), (False, chunks - 4),
+        (False, chunks - 2), (True, chunks - 4), (True, chunks - 2),
+    ]
+    y_order[-6:] = [
+        (False, chunks - 2), (True, chunks - 5), (False, chunks - 3),
+        (False, chunks - 1), (True, chunks - 3), (True, chunks - 1),
+    ]
     return x_order, y_order
 
 
@@ -263,7 +271,7 @@
 
     tile = 256
 
-    def multiply(at, slots, fresh=False, final=False, unroll=False):
+    def multiply(at, slots, fresh=False, final=False, unroll=True):
         @pl.loop(0, width // tile, unroll=unroll)
         def _(t):
             cols = pl.ds(pl.multiple_of(t * tile, tile), tile)
@@ -372,9 +380,9 @@
     up_event(0, 0)
     multiply_sides(1)
     event(6)
-    multiply_diagonal(1)
     event(7)
     up_event(0, 1)
+    multiply_diagonal(1)
     event(8)
     multiply_sides(2)
     event(9)
@@ -390,22 +398,15 @@
     multiply_sides(3)
     event(12)
     event(13)
+    event(14)
     multiply_diagonal(3)
-    event(14)
-    multiply_sides(4)
-    event(15)
     y_swap.wait_recv()
     sum_all[:, my_half, :] = (chip_part[...] + y_in[...].astype(jnp.float32)).astype(sum_all.dtype)
     sum_mate = single(sum_all.at[:, my_half, :], sum_all.at[:, my_half, :], "tp", mate)
-    event(16)
-    multiply_diagonal(blocks - 2)
-    multiply_sides(blocks - 1)
-    sum_mate.wait_recv()
-    for h in range(z_parts):
-        up_event(2, h)
-
-    last = blocks - 1
-    for b in range(blocks):
+    multiply_sides(blocks - 2)
+    event(15)
+
+    def add_adapted(b, final):
         at = of_block(b)
         adapted = lax.dot_general(
             sum_all[b],
@@ -414,12 +415,24 @@
             preferred_element_type=jnp.float32,
         )
         total = acc[at, :] + adapter_scale * adapted
-        if b < last:
+        if final:
             out_ref[at, :] = total.astype(out_ref.dtype)
         else:
             acc[at, :] = total
+
+    last = blocks - 1
+    sum_mate.wait_recv()
+    for h in range(z_parts):
+        up_event(reps - 2, h)
+    for b in range(blocks - 2):
+        add_adapted(b, True)
+    event(16)
+    multiply_sides(last)
     event(17)
+    multiply_diagonal(last - 1)
     multiply(of_block(last), (dg,), unroll=True)
+    add_adapted(last - 1, True)
+    add_adapted(last, False)
     wait_diagonal(last)
     multiply(of_block(last), (mate_of(dg),), final=True, unroll=True)
 

time: 43.8 us -> 41.5 us (0.947)
  Pallas kernels: 42.5 us -> 40.2 us
    pallas_call x1, Pallas kernels: 42.5 us -> 40.2 us  [shards(): pl.pallas_call(functools.partial(kernel, n, reps), out_shape=pltpu.VMEM((...]
where the time goes in v2:
time: 41.5 us; the launch traced here: 41.3 us
  Pallas kernels  40.2 us (97%)
  local copies, waits for them, and re-layouts  1.15 us (3%)
    pallas_call x1, Pallas kernels, shards(): pl.pallas_call(functools.partial(kernel, n, reps), out_shape=pltpu.VMEM((...  40.2 us
    unnamed x1, local copies, waits for them, and re-layouts  1.15 us

profile of v2, /device:TPU:0, one launch (start us, length us, event | category | flops | bytes accessed | tf_op | source)
XLA Modules:
  0.0 41.3 jit_solution(8244161781959390105)
XLA Ops:
  0.0 40.2 %shard_map.64 = bf16[768,1024]{1,0:T(8,128)(2,1)S(1)} custom-call(s32[6]{0:T(128)} %index_ref.1, s32[8]{0:T(128)} %table_ref.1, bf16[768,512]{1,0:T(8,128)(2,1)} %attn_ref.1, bf16[4096,1024]{1,0:T(8,128)(2,1)} %weight_ref.1, bf16[1,64,4096]{2,1,0:T(8,128)(2,1)} %down_ref.1, bf16[1,64,8192]{2,1,0:T(8,128)(2,1)} %up_ref.1), custom_call_target="tpu_custom_call" | custom-call | tf_op jit(solution)/shard_map/pallas_call | solution.py:461
  40.2 1.1 %copy.8 = bf16[768,1024]{1,0:T(8,128)(2,1)} copy(bf16[768,1024]{1,0:T(8,128)(2,1)S(1)} %shard_map.64) | data formatting | bytes 3145728

commit v3 on v2

--- a/solution.py
+++ b/solution.py
@@ -72,9 +72,8 @@
 
 
 def semaphore_counts(blocks, reps):
-    sends = 9 + 5 + 2 * z_parts * (reps - 1)
-    receives = 3 * blocks * split // 2 + 2 * blocks + 8 + 2 * z_parts * (reps - 1)
-    return sends, receives
+    receives = 3 * blocks * split // 2 + 2 * blocks + 9 + 2 * z_parts * (reps - 1)
+    return 13, receives
 
 
 def kernel(
@@ -94,8 +93,6 @@
     up_own,
     dn_all,
     up_all,
-    part,
-    half_in,
     chip_part,
     x_out,
     x_in,
@@ -111,7 +108,8 @@
     chunks = blocks * split
     rows = a_all.shape[1] // blocks
     chunk_rows = rows // split
-    rank = dn_all.shape[1]
+    half = dn_all.shape[1]
+    rank = 2 * half
     f_own = a_all.shape[2]
     c_own = up_all.shape[2]
     width = acc.shape[1]
@@ -124,7 +122,6 @@
     xn = me + 2 - 4 * x_at
     yn = me + 4 - 8 * y_at
     dg = xn + 4 - 8 * y_at
-    zp = z + 1 - 2 * lax.rem(z, 2)
 
     def mate_of(d):
         return d + 1 - 2 * core
@@ -163,20 +160,42 @@
         return copy
 
     quarter = rank // reps
-    pair_rank = rank // 2
+    z_bit = lax.rem(z, 2)
+    zp = z + 1 - 2 * z_bit
 
     def quarter_of(at):
         return pl.ds(pl.multiple_of(at * quarter, quarter), quarter)
 
+    eighth = f_own // 4
+    f_part = 3 * eighth
+    inner = (z == 1) | (z == 2)
+
+    def features(first, eighths):
+        return pl.ds(pl.multiple_of(first * eighth, eighth), eighths * eighth)
+
+    brought = z // 2 * 2 + (1 - z_bit) * 3
+
+    def quarter_from(plane):
+        return dn_all.at[:, :, features((plane - 1) * 6, 2)]
+
+    def half_of(at):
+        return pl.ds(pl.multiple_of(at * half, half), half)
+
+    def pages_of(h):
+        return pl.ds(h * (n // z_parts), n // z_parts)
+
+    my_half = half_of(core)
     up_rows = quarter_of(z)
-    dn_rows = pl.ds(pl.multiple_of(lax.rem(z, 2) * pair_rank, pair_rank), pair_rank)
-    own_f = pl.ds(pl.multiple_of(me * f_own, f_own), f_own)
     own_c = pl.ds(pl.multiple_of(me * c_own, c_own), c_own)
 
-    dn_stage = local(down_ref.at[0, dn_rows, :], dn_own)
+    dn_k = take("local")
+    for chip in range(n // 2):
+        local(down_ref.at[0, :, features(chip * 8 + brought, 3)], dn_own.at[:, features(chip * 3, 3)], dn_k)
     up_stage = local(up_ref.at[0, up_rows, :], up_own)
     own_load = local(attn_ref, a_all.at[me])
-    own_dn = local(down_ref.at[0, dn_rows, own_f], dn_all.at[me, dn_rows, :])
+    own_dn = local(
+        down_ref.at[0, my_half, features(me // 2 * 8 + brought, 3)], dn_all.at[me, :, features(brought, 3)]
+    )
     own_up = local(up_ref.at[0, up_rows, own_c], up_all.at[me, up_rows, :])
 
     barrier = pltpu.get_barrier_semaphore()
@@ -200,14 +219,14 @@
     up_s, up_r = take("send"), take("recv")
 
     def send_dn(j):
-        cols = pl.ds(pl.multiple_of(j * f_own, f_own), f_own)
-        remote(dn_own.at[:, cols], dn_all.at[me, dn_rows, :], "tp", j, dn_s, dn_r).start()
+        src = dn_own.at[half_of(lax.rem(j, 2)), features(j // 2 * 3, 3)]
+        remote(src, dn_all.at[me, :, features(brought, 3)], "tp", j, dn_s, dn_r).start()
 
     def send_up(j):
         cols = pl.ds(pl.multiple_of(j * c_own, c_own), c_own)
         remote(up_own.at[:, cols], up_all.at[me, up_rows, :], "tp", j, up_s, up_r).start()
 
-    dn_stage.wait()
+    drain(local_sem.at[dn_k], dn_own)
     for j in near:
         send_dn(j)
     pl.semaphore_wait(far_sem, 1)
@@ -222,17 +241,17 @@
         return a_all.at[slot, pl.ds(b * chunk_rows, chunk_rows), :]
 
     x_order, y_order = link_orders(chunks)
-    x_own, y_own, passed_on, x_pass, y_pass, d_pass = (take("send") for _ in range(6))
+    link_s, mate_s = take("send"), take("send")
     event_r, side_r, diag_r = take("recv", len(x_order)), take("recv", blocks), take("recv", blocks)
 
     def issue(k):
         if k < len(x_order):
             passed, b = x_order[k]
             src = chunk(yn if passed else me, b)
-            remote(src, src, "tp", xn, passed_on if passed else x_own, event_r + k).start()
+            remote(src, src, "tp", xn, link_s, event_r + k).start()
             passed, b = y_order[k]
             src = chunk(xn if passed else me, b)
-            remote(src, src, "tp", yn, passed_on if passed else y_own, event_r + k).start()
+            remote(src, src, "tp", yn, link_s, event_r + k).start()
 
     issued = [0]
 
@@ -253,10 +272,10 @@
     def event(k):
         drain(recv_sem.at[event_r + k], rows_of(2))
         issue_up_to(k)
-        for (passed, b), side, s in ((x_order[k], xn, x_pass), (y_order[k], yn, y_pass)):
+        for (passed, b), side in ((x_order[k], xn), (y_order[k], yn)):
             src = chunk(dg if passed else side, b)
             r = (diag_r if passed else side_r) + b // split
-            remote(src, src, "tp", mate, d_pass if passed else s, r).start()
+            remote(src, src, "tp", mate, mate_s, r).start()
 
     mate_copy = single(a_all.at[me], a_all.at[me], "tp", mate)
     issue_up_to(-1)
@@ -300,12 +319,48 @@
         wait_diagonal(b)
         multiply(of_block(b), (dg, mate_of(dg)), final=final)
 
-    half = rank // 2
-    my_half = pl.ds(pl.multiple_of(core * half, half), half)
-    mate_half = pl.ds(pl.multiple_of((1 - core) * half, half), half)
-
     def pages(b):
         return table_ref[index_ref[b]]
+
+    def line(piece_of, many):
+        sems = {True: take("send"), False: take("send")}
+        first = take("recv", 2 * z_parts * (reps - 1))
+
+        def copy(right, step, h):
+            piece = piece_of(z - step if right else z + step, h)
+            k = first + (step * 2 + (0 if right else 1)) * z_parts + h
+            return remote(piece, piece, "rep", z + 1 if right else z - 1, sems[right], k)
+
+        def start(step, h):
+            for right in (True, False):
+                @pl.when((z + 1 < reps) & (z >= step) if right else (z > 0) & (z + step < reps))
+                def _():
+                    copy(right, step, h).start()
+
+        def arrived(step, h):
+            for right in (True, False):
+                @pl.when(z > step if right else z + 1 + step < reps)
+                def _():
+                    copy(right, step, h).wait_recv()
+
+            if step + 1 < reps - 1:
+                start(step + 1, h)
+
+        def finish():
+            for right in (True, False):
+                for sent in range(1, reps):
+                    @pl.when(z == sent - 1 if right else z == reps - sent)
+                    def _():
+                        drain(send_sem.at[sems[right]], many(sent))
+
+        return start, arrived, finish
+
+    up_start, up_event, up_finish = line(
+        lambda owner, h: up_all.at[pages_of(h), quarter_of(owner), :],
+        lambda sent: up_all.at[:, pl.ds(0, sent * quarter), :],
+    )
+    dn_seven = dn_all.at[pl.ds(0, n - 1), :, pl.ds(0, f_part)]
+    up_seven = up_own.at[:, pl.ds(0, (n - 1) * c_own)]
 
     own_pairs = blocks // 2
     mate_copy.wait_recv()
@@ -314,67 +369,73 @@
         multiply(pl.ds(s * 2 * rows, 2 * rows), (me, mate), fresh=True)
         if s == 0:
             own_dn.wait()
-            drain(recv_sem.at[dn_r], dn_own.at[:, pl.ds(0, (n - 1) * f_own)])
-            dn_z = single(dn_all.at[:, dn_rows, :], dn_all.at[:, dn_rows, :], "rep", zp)
-
-    z_s, z_r = take("send", 2 * z_parts * (reps - 1)), take("recv", 2 * z_parts * (reps - 1))
-
-    def up_piece(owner, right, step, h):
-        pages_of = pl.ds(h * (n // z_parts), n // z_parts)
-        piece = up_all.at[pages_of, quarter_of(owner), :]
-        k = (step * 2 + (0 if right else 1)) * z_parts + h
-        return remote(piece, piece, "rep", z + 1 if right else z - 1, z_s + k, z_r + k)
-
-    def up_sends(right, step):
-        return (z + 1 < reps) & (z >= step) if right else (z > 0) & (z + step < reps)
-
-    def up_receives(right, step):
-        return z > step if right else z + 1 + step < reps
-
-    def up_owner(right, step):
-        return z - step if right else z + step
-
-    def up_start(step, h):
-        for right in (True, False):
-            @pl.when(up_sends(right, step))
+            drain(recv_sem.at[dn_r], dn_seven)
+            side = dn_all.at[:, :, features(brought, 3)]
+            dn_z = single(side, side, "rep", zp)
+            cross_s, cross_r, onward_s, onward_r = take("send"), take("recv"), take("send"), take("recv")
+
+            def cross(plane):
+                return remote(quarter_from(plane), quarter_from(plane), "rep", 3 - z, cross_s, cross_r)
+
+            def onward(plane):
+                return remote(quarter_from(plane), quarter_from(plane), "rep", zp, onward_s, onward_r)
+
+            @pl.when(inner)
             def _():
-                up_piece(up_owner(right, step), right, step, h).start()
-
-    def up_event(step, h):
-        for right in (True, False):
-            @pl.when(up_receives(right, step))
-            def _():
-                up_piece(up_owner(right, step), right, step, h).wait_recv()
-
-        if step + 1 < reps - 1:
-            up_start(step + 1, h)
-
+                cross(z).start()
     own_up.wait()
-    drain(recv_sem.at[up_r], up_own.at[:, pl.ds(0, (n - 1) * c_own)])
+    drain(recv_sem.at[up_r], up_seven)
+    for i in range(1, 4):
+        w_wait(i)
+
+    def add_adapted(b, final):
+        at = of_block(b)
+        adapted = lax.dot_general(
+            sum_all[b],
+            up_all[pages(b)],
+            (((0,), (0,)), ((), ())),
+            preferred_element_type=jnp.float32,
+        )
+        total = acc[at, :] + adapter_scale * adapted
+        if final:
+            out_ref[at, :] = total.astype(out_ref.dtype)
+        else:
+            acc[at, :] = total
+
+    last = blocks - 1
+    event(0)
+
+    @pl.when(inner)
+    def _():
+        cross(3 - z).wait_recv()
+        onward(3 - z).start()
+
     for h in range(z_parts):
         up_start(0, h)
-    for i in range(1, 4):
-        w_wait(i)
-
-    event(0)
     event(1)
     event(2)
     multiply_sides(0)
+    event(3)
     dn_z.wait_recv()
+
+    @pl.when(jnp.logical_not(inner))
+    def _():
+        onward(jnp.where(z == 0, 2, 1)).wait_recv()
+
     for b in range(blocks):
-        part[b] = lax.dot_general(
-            dn_all[pages(b)],
-            a_all[me, of_block(b), :],
-            (((1,), (1,)), ((), ())),
-            preferred_element_type=jnp.float32,
-        )
-    half_copy = single(part.at[:, mate_half, :], half_in, "tp", mate)
-    event(3)
+        page = pages(b)
+        for s in range(2):
+            term = lax.dot_general(
+                dn_all[page, :, pl.ds(s * f_own, f_own)],
+                a_all[me - core + s, of_block(b), :],
+                (((1,), (1,)), ((), ())),
+                preferred_element_type=jnp.float32,
+            )
+            total = term if s == 0 else total + term
+        chip_part[b] = total
+        x_out[b] = total.astype(x_out.dtype)
+    x_swap = single(x_out, x_in, "tp", xn)
     event(4)
-    half_copy.wait_recv()
-    chip_part[...] = part[:, my_half, :] + half_in[...]
-    x_out[...] = chip_part[...].astype(x_out.dtype)
-    x_swap = single(x_out, x_in, "tp", xn)
     multiply_diagonal(0)
     event(5)
     up_event(0, 0)
@@ -399,36 +460,21 @@
     event(12)
     event(13)
     event(14)
-    multiply_diagonal(3)
     y_swap.wait_recv()
     sum_all[:, my_half, :] = (chip_part[...] + y_in[...].astype(jnp.float32)).astype(sum_all.dtype)
     sum_mate = single(sum_all.at[:, my_half, :], sum_all.at[:, my_half, :], "tp", mate)
+    multiply_diagonal(3)
     multiply_sides(blocks - 2)
     event(15)
 
-    def add_adapted(b, final):
-        at = of_block(b)
-        adapted = lax.dot_general(
-            sum_all[b],
-            up_all[pages(b)],
-            (((0,), (0,)), ((), ())),
-            preferred_element_type=jnp.float32,
-        )
-        total = acc[at, :] + adapter_scale * adapted
-        if final:
-            out_ref[at, :] = total.astype(out_ref.dtype)
-        else:
-            acc[at, :] = total
-
-    last = blocks - 1
+    event(16)
+    multiply_sides(last)
+    event(17)
     sum_mate.wait_recv()
     for h in range(z_parts):
         up_event(reps - 2, h)
     for b in range(blocks - 2):
         add_adapted(b, True)
-    event(16)
-    multiply_sides(last)
-    event(17)
     multiply_diagonal(last - 1)
     multiply(of_block(last), (dg,), unroll=True)
     add_adapted(last - 1, True)
@@ -438,16 +484,16 @@
 
     for copy in singles:
         copy.wait_send()
-    drain(send_sem.at[dn_s], dn_own.at[:, pl.ds(0, (n - 1) * f_own)])
-    drain(send_sem.at[up_s], up_own.at[:, pl.ds(0, (n - 1) * c_own)])
-    for s in (x_own, y_own, passed_on, x_pass, y_pass, d_pass):
-        drain(send_sem.at[s], a_all.at[0])
-    for step in range(reps - 1):
-        for right in (True, False):
-            @pl.when(up_sends(right, step))
-            def _():
-                for h in range(z_parts):
-                    up_piece(up_owner(right, step), right, step, h).wait_send()
+    drain(send_sem.at[dn_s], dn_seven)
+    drain(send_sem.at[up_s], up_seven)
+    for s in (link_s, mate_s):
+        drain(send_sem.at[s], a_all.at[pl.ds(0, 3)])
+    up_finish()
+
+    @pl.when(inner)
+    def _():
+        cross(z).wait_send()
+        onward(3 - z).wait_send()
 
 
 def shards(n, reps, attn, weight, down, up, index, table):
@@ -468,12 +514,10 @@
             pltpu.VMEM((n, tokens, f_own), jnp.bfloat16),
             pltpu.VMEM((n, features // n, width), jnp.bfloat16),
             pltpu.VMEM((tokens, width), jnp.float32),
-            pltpu.VMEM((rank // 2, features), jnp.bfloat16),
+            pltpu.VMEM((rank, features // 8 * 3), jnp.bfloat16),
             pltpu.VMEM((rank // reps, n * width), jnp.bfloat16),
-            pltpu.VMEM((n, rank, f_own), jnp.bfloat16),
+            pltpu.VMEM((n, rank // 2, 2 * f_own), jnp.bfloat16),
             pltpu.VMEM((n, rank, width), jnp.bfloat16),
-            pltpu.VMEM((blocks, rank, rows), jnp.float32),
-            pltpu.VMEM(half, jnp.float32),
             pltpu.VMEM(half, jnp.float32),
             pltpu.VMEM(half, jnp.bfloat16),
             pltpu.VMEM(half, jnp.bfloat16),
@@ -505,7 +549,7 @@
             and down.shape[1] % (16 * reps) == 0
             and down.shape[1] % (8 * n) == 0
             and attn.shape[0] % (128 * blocks) == 0
-            and attn.shape[1] % 128 == 0
+            and attn.shape[1] % 512 == 0
             and weight.shape[1] % 256 == 0
         )
         if fits:

time: 41.5 us -> 41.2 us (level)
  no operation moved by 1% of the time
where the time goes in v3:
time: 41.2 us; the launch traced here: 41 us
  Pallas kernels  39.9 us (97%)
  local copies, waits for them, and re-layouts  1.15 us (3%)
    pallas_call x1, Pallas kernels, shards(): pl.pallas_call(functools.partial(kernel, n, reps), out_shape=pltpu.VMEM((...  39.9 us
    unnamed x1, local copies, waits for them, and re-layouts  1.15 us

profile of v3, /device:TPU:0, one launch (start us, length us, event | category | flops | bytes accessed | tf_op | source)
XLA Modules:
  0.0 41.0 jit_solution(11807602645290692852)
XLA Ops:
  0.0 39.9 %shard_map.64 = bf16[768,1024]{1,0:T(8,128)(2,1)S(1)} custom-call(s32[6]{0:T(128)} %index_ref.1, s32[8]{0:T(128)} %table_ref.1, bf16[768,512]{1,0:T(8,128)(2,1)} %attn_ref.1, bf16[4096,1024]{1,0:T(8,128)(2,1)} %weight_ref.1, bf16[1,64,4096]{2,1,0:T(8,128)(2,1)} %down_ref.1, bf16[1,64,8192]{2,1,0:T(8,128)(2,1)} %up_ref.1), custom_call_target="tpu_custom_call" | custom-call | tf_op jit(solution)/shard_map/pallas_call | solution.py:507
  39.9 1.1 %copy.8 = bf16[768,1024]{1,0:T(8,128)(2,1)} copy(bf16[768,1024]{1,0:T(8,128)(2,1)S(1)} %shard_map.64) | data formatting | bytes 3145728

commit v4 on v3

--- a/solution.py
+++ b/solution.py
@@ -72,7 +72,7 @@
 
 
 def semaphore_counts(blocks, reps):
-    receives = 3 * blocks * split // 2 + 2 * blocks + 9 + 2 * z_parts * (reps - 1)
+    receives = 2 * depth + 1 + 2 * blocks + 9 + 2 * z_parts * (reps - 1)
     return 13, receives
 
 
@@ -191,42 +191,41 @@
     dn_k = take("local")
     for chip in range(n // 2):
         local(down_ref.at[0, :, features(chip * 8 + brought, 3)], dn_own.at[:, features(chip * 3, 3)], dn_k)
+    barrier = pltpu.get_barrier_semaphore()
+    near = (xn, yn, mate_of(xn), mate_of(yn), mate)
+    for d in near:
+        pl.semaphore_signal(barrier, inc=1, device_id={"tp": d}, device_id_type=MESH)
+
+    @pl.when(z + 1 < reps)
+    def _():
+        pl.semaphore_signal(barrier, inc=1, device_id={"rep": z + 1}, device_id_type=MESH)
+
+    @pl.when(z > 0)
+    def _():
+        pl.semaphore_signal(barrier, inc=1, device_id={"rep": z - 1}, device_id_type=MESH)
+
+    z_near = jnp.where(z > 0, 1, 0) + jnp.where(z + 1 < reps, 1, 0)
+    pl.semaphore_wait(barrier, len(near) + z_near)
+    pl.semaphore_signal(far_sem, inc=1, device_id={"tp": xn}, device_id_type=MESH)
+
+    dn_s, dn_r = take("send"), take("recv")
+    up_s, up_r = take("send"), take("recv")
+
+    def send_dn(j):
+        src = dn_own.at[half_of(lax.rem(j, 2)), features(j // 2 * 3, 3)]
+        remote(src, dn_all.at[me, :, features(brought, 3)], "tp", j, dn_s, dn_r).start()
+
+    def send_up(j):
+        cols = pl.ds(pl.multiple_of(j * c_own, c_own), c_own)
+        remote(up_own.at[:, cols], up_all.at[me, up_rows, :], "tp", j, up_s, up_r).start()
+
+    drain(local_sem.at[dn_k], dn_own)
     up_stage = local(up_ref.at[0, up_rows, :], up_own)
     own_load = local(attn_ref, a_all.at[me])
     own_dn = local(
         down_ref.at[0, my_half, features(me // 2 * 8 + brought, 3)], dn_all.at[me, :, features(brought, 3)]
     )
     own_up = local(up_ref.at[0, up_rows, own_c], up_all.at[me, up_rows, :])
-
-    barrier = pltpu.get_barrier_semaphore()
-    near = (xn, yn, mate_of(xn), mate_of(yn), mate)
-    for d in near:
-        pl.semaphore_signal(barrier, inc=1, device_id={"tp": d}, device_id_type=MESH)
-
-    @pl.when(z + 1 < reps)
-    def _():
-        pl.semaphore_signal(barrier, inc=1, device_id={"rep": z + 1}, device_id_type=MESH)
-
-    @pl.when(z > 0)
-    def _():
-        pl.semaphore_signal(barrier, inc=1, device_id={"rep": z - 1}, device_id_type=MESH)
-
-    z_near = jnp.where(z > 0, 1, 0) + jnp.where(z + 1 < reps, 1, 0)
-    pl.semaphore_wait(barrier, len(near) + z_near)
-    pl.semaphore_signal(far_sem, inc=1, device_id={"tp": xn}, device_id_type=MESH)
-
-    dn_s, dn_r = take("send"), take("recv")
-    up_s, up_r = take("send"), take("recv")
-
-    def send_dn(j):
-        src = dn_own.at[half_of(lax.rem(j, 2)), features(j // 2 * 3, 3)]
-        remote(src, dn_all.at[me, :, features(brought, 3)], "tp", j, dn_s, dn_r).start()
-
-    def send_up(j):
-        cols = pl.ds(pl.multiple_of(j * c_own, c_own), c_own)
-        remote(up_own.at[:, cols], up_all.at[me, up_rows, :], "tp", j, up_s, up_r).start()
-
-    drain(local_sem.at[dn_k], dn_own)
     for j in near:
         send_dn(j)
     pl.semaphore_wait(far_sem, 1)
@@ -242,16 +241,17 @@
 
     x_order, y_order = link_orders(chunks)
     link_s, mate_s = take("send"), take("send")
-    event_r, side_r, diag_r = take("recv", len(x_order)), take("recv", blocks), take("recv", blocks)
+    ring = 2 * depth + 1
+    event_r, side_r, diag_r = take("recv", ring), take("recv", blocks), take("recv", blocks)
 
     def issue(k):
         if k < len(x_order):
             passed, b = x_order[k]
             src = chunk(yn if passed else me, b)
-            remote(src, src, "tp", xn, link_s, event_r + k).start()
+            remote(src, src, "tp", xn, link_s, event_r + k % ring).start()
             passed, b = y_order[k]
             src = chunk(xn if passed else me, b)
-            remote(src, src, "tp", yn, link_s, event_r + k).start()
+            remote(src, src, "tp", yn, link_s, event_r + k % ring).start()
 
     issued = [0]
 
@@ -270,7 +270,7 @@
         return a_all.at[0, pl.ds(0, many * chunk_rows), :]
 
     def event(k):
-        drain(recv_sem.at[event_r + k], rows_of(2))
+        drain(recv_sem.at[event_r + k % ring], rows_of(2))
         issue_up_to(k)
         for (passed, b), side in ((x_order[k], xn), (y_order[k], yn)):
             src = chunk(dg if passed else side, b)
@@ -475,10 +475,10 @@
         up_event(reps - 2, h)
     for b in range(blocks - 2):
         add_adapted(b, True)
-    multiply_diagonal(last - 1)
+    add_adapted(last, False)
+    add_adapted(last - 1, False)
+    multiply_diagonal(last - 1, final=True)
     multiply(of_block(last), (dg,), unroll=True)
-    add_adapted(last - 1, True)
-    add_adapted(last, False)
     wait_diagonal(last)
     multiply(of_block(last), (mate_of(dg),), final=True, unroll=True)
 

time: 41.2 us -> 41 us (level)
  no operation moved by 1% of the time
where the time goes in v4:
time: 41 us; the launch traced here: 40.8 us
  Pallas kernels  39.7 us (97%)
  local copies, waits for them, and re-layouts  1.15 us (3%)
    pallas_call x1, Pallas kernels, shards(): pl.pallas_call(functools.partial(kernel, n, reps), out_shape=pltpu.VMEM((...  39.7 us
    unnamed x1, local copies, waits for them, and re-layouts  1.15 us

profile of v4, /device:TPU:0, one launch (start us, length us, event | category | flops | bytes accessed | tf_op | source)
XLA Modules:
  0.0 40.8 jit_solution(13549001866398281301)
XLA Ops:
  0.0 39.7 %shard_map.64 = bf16[768,1024]{1,0:T(8,128)(2,1)S(1)} custom-call(s32[6]{0:T(128)} %index_ref.1, s32[8]{0:T(128)} %table_ref.1, bf16[768,512]{1,0:T(8,128)(2,1)} %attn_ref.1, bf16[4096,1024]{1,0:T(8,128)(2,1)} %weight_ref.1, bf16[1,64,4096]{2,1,0:T(8,128)(2,1)} %down_ref.1, bf16[1,64,8192]{2,1,0:T(8,128)(2,1)} %up_ref.1), custom_call_target="tpu_custom_call" | custom-call | tf_op jit(solution)/shard_map/pallas_call | solution.py:507
  39.7 1.1 %copy.8 = bf16[768,1024]{1,0:T(8,128)(2,1)} copy(bf16[768,1024]{1,0:T(8,128)(2,1)S(1)} %shard_map.64) | data formatting | bytes 3145728
